TPU v7x, 512 devices: a whole 4x8x8 slice. The times are simulated.
512 devices in a mesh: blk: 64 (over z, y_hi, core), rep: 8 (over y_lo, x).
Axes of the slice: x: 4, y: 8 (y_hi: 4, y_lo: 2; y = y_hi * 2 + y_lo), z: 8, core: 2. Of those that a mesh axis runs over, the one named last changes fastest.
Arguments:
- raw_integrals: float32 [64, 1024, 512], P(None, 'blk'), may hold values from -0.6 to 0.6
- virtual_coeffs: float32 [512, 256], P(None, 'rep'), may hold values from -0.25 to 0.25
- metric_root: float32 [1024, 1024], P(None, 'rep'), may hold values from -1 to 3, as said below
- occ_energies: float32 [64], P('blk'), may hold values from -2 to -0.5
- virt_energies: float32 [256], replicated, may hold values from 0.2 to 3
Outputs:
- gamma: float32 [64, 256, 1024], P('blk', None, 'rep')
Inputs may be any that keep to these rules, and one draw needn't show every extreme that they name: metric_root is exactly symmetric.
All inputs are finite; a program needn't handle non-finite values.
Results may differ from a plain program's by a relative error of at most 0.0001.
Values sent between devices are 32-bit elements; how exact they have to be, the bound alone decides.
A program may use at most 64 MiB of HBM per device.

v0:
```python
import jax
import jax.numpy as jnp
from jax import lax
from jax.sharding import Mesh
from jax.sharding import PartitionSpec as P

TURNS = 2
BLK = ("blk_0", "blk_1", "blk_2")


def split_up(x, dim, count):
    lengths = x.shape
    parts = x.reshape(*lengths[:dim], count, lengths[dim] // count, *lengths[dim + 1 :])
    return jnp.moveaxis(parts, dim, 0)


def laid_out(parts, dim):
    lengths = list(parts.shape[1:])
    lengths[dim] *= parts.shape[0]
    return jnp.moveaxis(parts, 0, dim).reshape(lengths)


def turned_blocks(parts, axes, turns):
    inside = parts.shape[1:]
    filled = parts.reshape(*(lax.axis_size(a) for a in axes), *inside)
    for k in turns:
        filled = lax.all_to_all(filled, axes[k], k, k, tiled=True)
    return filled.reshape(-1, *inside)


def core_and_chips(x, groups, turns, split_dim, concat_dim):
    count = lax.axis_size(groups[0]) * lax.axis_size(groups[1])
    parts = split_up(x, split_dim, count)
    return laid_out(turned_blocks(parts, groups, turns), concat_dim)


def copy_for_each(x, axis):
    copies = jnp.broadcast_to(x, (lax.axis_size(axis), *x.shape))
    return lax.all_to_all(copies, axis, split_axis=0, concat_axis=0, tiled=True)


def collect(x, axis, dim):
    return laid_out(copy_for_each(x, axis), dim)


def from_behind(x, axis, by):
    count = lax.axis_size(axis)
    return lax.ppermute(x, axis, [(i, (i + by) % count) for i in range(count)])


def summed_on_arrival(x, axis, dim):
    parts = split_up(x, dim, lax.axis_size(axis))
    arrived = lax.all_to_all(parts, axis, split_axis=0, concat_axis=0, tiled=True)
    return arrived.sum(axis=0)


def pair_terms(own_rows, own_eps, other_rows, other_eps, virt_energies, gradient):
    highest = lax.Precision.HIGHEST
    coulomb = jnp.einsum("xaq,ybq->xyab", own_rows, other_rows, precision=highest)
    spread = virt_energies[:, None] + virt_energies[None, :]
    denominator = spread[None, None] - own_eps[:, None, None, None] - other_eps[None, :, None, None]
    amplitude = (2.0 * coulomb - jnp.swapaxes(coulomb, 2, 3)) / denominator
    return gradient + jnp.einsum("xyab,ybq->xaq", amplitude, other_rows, precision=highest)


def per_device(raw_integrals, virtual_coeffs, metric_root, occ_energies, virt_energies):
    highest = lax.Precision.HIGHEST
    halfway = jnp.einsum("ipm,ma->ipa", raw_integrals, virtual_coeffs, precision=highest)
    regrouped = core_and_chips(halfway, (("blk_0", "blk_1"), "blk_2"), (1, 0), 0, 1)
    complete = collect(regrouped, "rep", 2)
    fitted_part = jnp.einsum("xpa,pq->xaq", complete, metric_root, precision=highest)
    fitted = collect(fitted_part, "rep", 2)
    replica = lax.axis_index("rep")
    replicas = lax.axis_size("rep")
    turns = TURNS
    turn_unit = 1
    travel_rows = fitted
    travel_eps = occ_energies
    for bit_index in range((replicas - 1).bit_length()):
        shifted_rows, shifted_eps = from_behind(
            (travel_rows, travel_eps), BLK, (1 << bit_index) * turns
        )
        chosen = replica >> bit_index & 1 == 1
        travel_rows = jnp.where(chosen, shifted_rows, travel_rows)
        travel_eps = jnp.where(chosen, shifted_eps, travel_eps)
    gradient = jnp.zeros(fitted.shape, jnp.float32)

    def advance(turn_index, state_now):
        other_rows, other_eps, total = state_now
        total = pair_terms(fitted, occ_energies, other_rows, other_eps, virt_energies, total)
        other_rows, other_eps = from_behind((other_rows, other_eps), BLK, turn_unit)
        return (other_rows, other_eps, total)

    travel_rows, travel_eps, gradient = lax.fori_loop(
        0, turns - 1, advance, (travel_rows, travel_eps, gradient)
    )
    gradient = pair_terms(fitted, occ_energies, travel_rows, travel_eps, virt_energies, gradient)
    return summed_on_arrival(gradient, "rep", 2)


def solution(mesh):
    finer = Mesh(
        mesh.devices.reshape(8, 4, 2, mesh.shape["rep"]), ("blk_0", "blk_1", "blk_2", "rep")
    )
    return jax.shard_map(
        per_device,
        mesh=finer,
        in_specs=(P(None, BLK, None), P(None, "rep"), P(None, "rep"), P(BLK), P()),
        out_specs=P(BLK, None, "rep"),
        check_vma=False,
    )
```

profile of v0, /device:TPU:1, one launch (start us, length us, event | category | flops | bytes accessed | tf_op | source)
XLA Modules:
  0.0 293.5 jit_solution(8197330092977087505)
XLA Ops:
  1.6 2.6 fusion.30
  4.5 10.3 %all_to_all.25 = f32[2,1,16384]{2,1,0:T(1,128)S(1)} all-to-all(f32[2,1,16384]{2,1,0:T(1,128)S(1)} %reshape.159), channel_id=1, replica_groups=mesh['blk_0'=8,'blk_1'=4,'blk_2'=2,'rep'=8] {'blk_2'}, dimensions={0} | all-to-all | bytes 262144 | tf_op jit(solution)/shard_map/all_to_all | solution.py:27
  16.9 21.5 %all_to_all.26 = f32[32,1,1024]{2,1,0:T(1,128)S(1)} all-to-all(f32[32,1,1024]{2,1,0:T(1,128)S(1)} %reshape.161), channel_id=1, replica_groups=mesh['blk_0'=8,'blk_1'=4,'blk_2'=2,'rep'=8] {'blk_0','blk_1'}, dimensions={0} | all-to-all | bytes 262144 | tf_op jit(solution)/shard_map/all_to_all | solution.py:27
  39.8 17.0 %all_to_all.27 = f32[8,1,1024,32]{2,3,1,0:T(8,128)S(1)} all-to-all(f32[8,1,1024,32]{2,3,1,0:T(8,128)S(1)} %broadcast_in_dim.14), channel_id=1, replica_groups=mesh['blk_0'=8,'blk_1'=4,'blk_2'=2,'rep'=8] {'rep'}, dimensions={0} | all-to-all | bytes 2097152 | tf_op jit(solution)/shard_map/all_to_all | solution.py:39
  57.9 15.1 %all_to_all.28 = f32[8,1,256,128]{3,2,1,0:T(8,128)} all-to-all(f32[8,1,256,128]{3,2,1,0:T(8,128)S(1)} %broadcast_in_dim.15), channel_id=1, replica_groups=mesh['blk_0'=8,'blk_1'=4,'blk_2'=2,'rep'=8] {'rep'}, dimensions={0} | all-to-all | bytes 2097152 | tf_op jit(solution)/shard_map/all_to_all | solution.py:39
  74.6 1.9 collective-permute-start
  76.5 30.2 %collective-permute-done = f32[1,256,1024]{1,2,0:T(8,128)} collective-permute-done((f32[1,256,1024]{1,2,0:T(8,128)S(1)}, f32[1,256,1024]{1,2,0:T(8,128)}, u32[]{:S(2)}, u32[]{:S(2)}) %collective-permute-start) | collective-permute-done | bytes 1048608 | tf_op jit(solution)/shard_map/ppermute | solution.py:48
  108.0 5.8 %collective-permute-start.1 = (f32[1,256,1024]{1,2,0:T(8,128)}, f32[1,256,1024]{1,2,0:T(8,128)}, u32[]{:S(2)}, u32[]{:S(2)}) collective-permute-start(f32[1,256,1024]{1,2,0:T(8,128)} %broadcast_select_fusion), channel_id=1, source_target_pairs={{0,32},{8,40},{16,48},{24,56},{32,64},{40,72},{48,80},{56,88},{64,... | collective-permute-start | bytes 3145736 | tf_op jit(solution)/shard_map/ppermute | solution.py:48
  113.8 54.7 %collective-permute-done.1 = f32[1,256,1024]{1,2,0:T(8,128)} collective-permute-done((f32[1,256,1024]{1,2,0:T(8,128)}, f32[1,256,1024]{1,2,0:T(8,128)}, u32[]{:S(2)}, u32[]{:S(2)}) %collective-permute-start.1) | collective-permute-done | bytes 1048608 | tf_op jit(solution)/shard_map/ppermute | solution.py:48
  168.5 2.4 broadcast_select_fusion.1
  172.8 21.8 %collective-permute-done.2 = f32[1,256,1024]{1,2,0:T(8,128)} collective-permute-done((f32[1,256,1024]{1,2,0:T(8,128)}, f32[1,256,1024]{1,2,0:T(8,128)}, u32[]{:S(2)}, u32[]{:S(2)}) %collective-permute-start.2) | collective-permute-done | bytes 1048608 | tf_op jit(solution)/shard_map/ppermute | solution.py:48
  194.6 2.4 broadcast_select_fusion.2
  197.0 8.8 %collective-permute-start.6 = (f32[1,256,1024]{1,2,0:T(8,128)}, f32[1,256,1024]{1,2,0:T(8,128)}, u32[]{:S(2)}, u32[]{:S(2)}) collective-permute-start(f32[1,256,1024]{1,2,0:T(8,128)} %broadcast_select_fusion.2), channel_id=1, source_target_pairs={{0,8},{8,16},{16,24},{24,32},{32,40},{40,48},{48,56},{56,64},{64,7... | collective-permute-start | bytes 3145736 | tf_op jit(solution)/shard_map/while/body/eval_jaxpr/ppermute | solution.py:48
  205.8 7.2 %collective-permute-start.3 = (f32[1]{0:T(128)}, f32[1]{0:T(128)}, u32[]{:S(2)}, u32[]{:S(2)}) collective-permute-start(f32[1]{0:T(128)} %param.8), channel_id=1, source_target_pairs={{0,16},{8,24},{16,32},{24,40},{32,48},{40,56},{48,64},{56,72},{64,... | collective-permute-start | bytes 20 | tf_op jit(solution)/shard_map/ppermute | solution.py:48
  213.7 9.8 %collective-permute-done.3 = f32[1]{0:T(128)} collective-permute-done((f32[1]{0:T(128)}, f32[1]{0:T(128)}, u32[]{:S(2)}, u32[]{:S(2)}) %collective-permute-start.3) | collective-permute-done | bytes 36 | tf_op jit(solution)/shard_map/ppermute | solution.py:48
  224.2 17.6 %collective-permute-start.4 = (f32[1]{0:T(128)}, f32[1]{0:T(128)}, u32[]{:S(2)}, u32[]{:S(2)}) collective-permute-start(f32[1]{0:T(128)} %select_n.49), channel_id=1, source_target_pairs={{0,32},{8,40},{16,48},{24,56},{32,64},{40,72},{48,80},{56,88},{64,... | collective-permute-start | bytes 20 | tf_op jit(solution)/shard_map/ppermute | solution.py:48
  243.9 2.7 collective-permute-start.5
  246.6 4.1 %collective-permute-done.5 = f32[1]{0:T(128)} collective-permute-done((f32[1]{0:T(128)}, f32[1]{0:T(128)}, u32[]{:S(2)}, u32[]{:S(2)}) %collective-permute-start.5) | collective-permute-done | bytes 36 | tf_op jit(solution)/shard_map/ppermute | solution.py:48
  251.3 2.6 collective-permute-start.7
  254.0 3.0 %fusion.6 = f32[256,256]{1,0:T(8,128)S(1)} fusion(f32[256,1024]{0,1:T(8,128)S(1)} %bitcast.93, f32[1,256,1024]{1,2,0:T(8,128)} %broadcast_select_fusion.2), kind=kOutput, calls=%fused_computation.7 | convolution fusion | flops 805306368 | bytes 2359296 | tf_op jit(solution)/shard_map/while/body/eval_jaxpr/xaq,ybq->xyab/dot_general | solution.py:59
  257.9 3.7 %fusion.3 = f32[256,256]{1,0:T(8,128)} fusion(f32[256,1024]{0,1:T(8,128)S(1)} %bitcast.94, f32[1,256,1024]{1,2,0:T(8,128)} %collective-permute-done.6), kind=kOutput, calls=%fused_computation.4 | convolution fusion | flops 805306368 | bytes 2359296 | tf_op jit(solution)/shard_map/xaq,ybq->xyab/dot_general | solution.py:59
  262.8 3.1 %fusion.1 = f32[256,1024]{1,0:T(8,128)S(1)} fusion(f32[1,256,1024]{1,2,0:T(8,128)} %collective-permute-done.6, f32[256,256]{1,0:T(8,128)} %fusion.3, f32[256,256]{0,1:T(8,128)S(1)} %copy.28, f32[]{:T(128)} %bitcast.25, f32[]{:T(128)} %bitcast.91, f32[256]{0:T(256)S(1)} %copy-done.3), kind=kOutput, calls=%fused_computation.2 | convolution fusion | flops 805699584 | bytes 2622472 | tf_op jit(solution)/shard_map/xyab,ybq->xaq/dot_general | solution.py:63
  265.9 2.3 fusion
  268.6 24.2 %all_to_all.29 = f32[8,1,256,128]{3,2,1,0:T(8,128)S(1)} all-to-all(f32[8,1,256,128]{3,2,1,0:T(8,128)S(1)} %bitcast.96), channel_id=1, replica_groups=mesh['blk_0'=8,'blk_1'=4,'blk_2'=2,'rep'=8] {'rep'}, dimensions={0} | all-to-all | bytes 2097152 | tf_op jit(solution)/shard_map/all_to_all | solution.py:53
  (32 shorter events, 15.7 us)
Async XLA Ops:
  0.0 1.6 copy-start
  39.5 17.3 %copy-start.2 = (f32[1024,128]{1,0:T(8,128)S(1)}, f32[1024,128]{1,0:T(8,128)}, u32[]{:S(2)}) copy-start(f32[1024,128]{1,0:T(8,128)} %param.7) | copy-start | bytes 1572868
  74.6 32.2 %collective-permute-start = (f32[1,256,1024]{1,2,0:T(8,128)S(1)}, f32[1,256,1024]{1,2,0:T(8,128)}, u32[]{:S(2)}, u32[]{:S(2)}) collective-permute-start(f32[1,256,1024]{1,2,0:T(8,128)S(1)} %bitcast.92), channel_id=1, source_target_pairs={{0,16},{8,24},{16,32},{24,40},{32,48},{40,56},{48,64},{56,72},{64,... | collective-permute-start | bytes 3145736 | tf_op jit(solution)/shard_map/ppermute | solution.py:48
  108.0 60.6 %collective-permute-start.1 = (f32[1,256,1024]{1,2,0:T(8,128)}, f32[1,256,1024]{1,2,0:T(8,128)}, u32[]{:S(2)}, u32[]{:S(2)}) collective-permute-start(f32[1,256,1024]{1,2,0:T(8,128)} %broadcast_select_fusion), channel_id=1, source_target_pairs={{0,32},{8,40},{16,48},{24,56},{32,64},{40,72},{48,80},{56,88},{64,... | collective-permute-start | bytes 3145736 | tf_op jit(solution)/shard_map/ppermute | solution.py:48
  170.9 23.7 %collective-permute-start.2 = (f32[1,256,1024]{1,2,0:T(8,128)}, f32[1,256,1024]{1,2,0:T(8,128)}, u32[]{:S(2)}, u32[]{:S(2)}) collective-permute-start(f32[1,256,1024]{1,2,0:T(8,128)} %broadcast_select_fusion.1), channel_id=1, source_target_pairs={{0,64},{8,72},{16,80},{24,88},{32,96},{40,104},{48,112},{56,120},{... | collective-permute-start | bytes 3145736 | tf_op jit(solution)/shard_map/ppermute | solution.py:48
  197.0 60.9 %collective-permute-start.6 = (f32[1,256,1024]{1,2,0:T(8,128)}, f32[1,256,1024]{1,2,0:T(8,128)}, u32[]{:S(2)}, u32[]{:S(2)}) collective-permute-start(f32[1,256,1024]{1,2,0:T(8,128)} %broadcast_select_fusion.2), channel_id=1, source_target_pairs={{0,8},{8,16},{16,24},{24,32},{32,40},{40,48},{48,56},{56,64},{64,7... | collective-permute-start | bytes 3145736 | tf_op jit(solution)/shard_map/while/body/eval_jaxpr/ppermute | solution.py:48
  205.8 17.7 %collective-permute-start.3 = (f32[1]{0:T(128)}, f32[1]{0:T(128)}, u32[]{:S(2)}, u32[]{:S(2)}) collective-permute-start(f32[1]{0:T(128)} %param.8), channel_id=1, source_target_pairs={{0,16},{8,24},{16,32},{24,40},{32,48},{40,56},{48,64},{56,72},{64,... | collective-permute-start | bytes 20 | tf_op jit(solution)/shard_map/ppermute | solution.py:48
  224.2 19.0 %collective-permute-start.4 = (f32[1]{0:T(128)}, f32[1]{0:T(128)}, u32[]{:S(2)}, u32[]{:S(2)}) collective-permute-start(f32[1]{0:T(128)} %select_n.49), channel_id=1, source_target_pairs={{0,32},{8,40},{16,48},{24,56},{32,64},{40,72},{48,80},{56,88},{64,... | collective-permute-start | bytes 20 | tf_op jit(solution)/shard_map/ppermute | solution.py:48
  243.9 6.8 %collective-permute-start.5 = (f32[1]{0:T(128)}, f32[1]{0:T(128)}, u32[]{:S(2)}, u32[]{:S(2)}) collective-permute-start(f32[1]{0:T(128)} %select_n.50), channel_id=1, source_target_pairs={{0,64},{8,72},{16,80},{24,88},{32,96},{40,104},{48,112},{56,120},{... | collective-permute-start | bytes 20 | tf_op jit(solution)/shard_map/ppermute | solution.py:48
  251.3 11.4 %collective-permute-start.7 = (f32[1]{0:T(128)}, f32[1]{0:T(128)}, u32[]{:S(2)}, u32[]{:S(2)}) collective-permute-start(f32[1]{0:T(128)} %select_n.51), channel_id=1, source_target_pairs={{0,8},{8,16},{16,24},{24,32},{32,40},{40,48},{48,56},{56,64},{64,7... | collective-permute-start | bytes 20 | tf_op jit(solution)/shard_map/while/body/eval_jaxpr/ppermute | solution.py:48
  257.0 5.8 %copy-start.3 = (f32[256]{0:T(256)S(1)}, f32[256]{0:T(256)}, u32[]{:S(2)}) copy-start(f32[256]{0:T(256)} %param.9) | copy-start | bytes 3076
  261.6 4.2 %copy-start.1 = (f32[256,256]{0,1:T(8,128)S(1)}, f32[256,256]{0,1:T(8,128)}, u32[]{:S(2)}) copy-start(f32[256,256]{0,1:T(8,128)} %copy.26) | copy-start | bytes 786436
where the time goes:
time: 295 us; the launch traced here: 294 us
  waiting for transfers between devices  122 us (41%)
  blocking collectives  88.2 us (30%)
  starting transfers between devices  48.5 us (16%)
  matrix products  15.8 us (5%)
  other arithmetic  8.66 us (3%)
  local copies, waits for them, and re-layouts  7.41 us (3%)
    ppermute x8, waiting for transfers between devices, from_behind(): return lax.ppermute(x, axis, [(i, (i + by) % count) for i in range(count)])  122 us
    ppermute x8, starting transfers between devices, from_behind(): return lax.ppermute(x, axis, [(i, (i + by) % count) for i in range(count)])  48.5 us
    all_to_all x2, blocking collectives, copy_for_each(): return lax.all_to_all(copies, axis, split_axis=0, concat_axis=0, tiled=True)  32.1 us
    all_to_all x2, blocking collectives, turned_blocks(): filled = lax.all_to_all(filled, axes[k], k, k, tiled=True)  31.8 us
    all_to_all x1, blocking collectives, summed_on_arrival(): lax.all_to_all(parts, axis, split_axis=0, concat_axis=0, tiled=True)  24.2 us
    dot_general x2, matrix products, pair_terms(): jnp.einsum('xaq,ybq->xyab', own_rows, other_rows, precision=highest)  6.79 us
    select_n x3, other arithmetic, per_device(): travel_rows = jnp.where(chosen, shifted_rows, travel_rows)  5.98 us
  transfers between devices with their start and end apart: 8, of which 6 were waited for; matrix products, arithmetic and copies ran while one was open for 3% of the time, Pallas kernels for 0%

commit v1 on v0

v1 whole, which is shorter than its diff:
```python
import jax
import jax.numpy as jnp
from jax import lax
from jax.experimental import pallas as pl
from jax.experimental.pallas import tpu as pltpu
from jax.sharding import Mesh
from jax.sharding import PartitionSpec as P

F32 = jnp.float32
BF16 = jnp.bfloat16
MESH = pl.DeviceIdType.MESH
Z, YH, CO, YL, X = 8, 4, 2, 2, 4
BLK = ("z", "yh", "co")
REP = ("yl", "x")
NI, NP, NM, NA, NQ = 64, 16, 512, 32, 128
HOLDER = (0, 1, 3, 4, 6, 2, 7, 5)
DISTANCE = (0, 1, 5, 2, 3, 7, 4, 6)


def halves(v):
    high = v.astype(BF16)
    return high, (v - high.astype(F32)).astype(BF16)


def mm(a, b):
    return jnp.dot(a, b, preferred_element_type=F32)


def mm3(a, b):
    return mm(a[0], b[0]) + (mm(a[0], b[1]) + mm(a[1], b[0]))


def mm_nt(a, b):
    return lax.dot_general(a, b, (((1,), (1,)), ((), ())), preferred_element_type=F32)


def strided(ref, count, k):
    parts = []
    for part in range(count):
        rows = [ref[part, pl.ds(4 * p + k, NI, stride=NP), :] for p in range(4)]
        parts.append(jnp.concatenate(rows, axis=0))
    return jnp.concatenate(parts, axis=1)


def pick(index, table):
    out = table[-1]
    for at in range(len(table) - 2, -1, -1):
        out = jnp.where(index == at, table[at], out)
    return jnp.int32(out)


def kernel(
    raw_hbm, c_ref, m_hbm, occ_ref, virt_ref, out_ref,
    raw_v, mbuf, hsend, hx, sbuf, fbuf, jhi, jlo, thi, tlo, esend, ebuf, g, grecv,
    local_sem, a2a_send, a2a_recv, m_send, m_recv, e_send, e_recv, x_send, x_recv,
    s_send, s_recv, f_send, f_recv, p_send, d_send, d_recv, g_send, g_recv,
):
    z, yh, co = lax.axis_index("z"), lax.axis_index("yh"), lax.axis_index("co")
    yl, x = lax.axis_index("yl"), lax.axis_index("x")
    me = (z * YH + yh) * CO + co
    chip = z * YH + yh
    rep = yl * X + x
    is_root = rep == HOLDER[0]

    def remote(src, dst, ss, rs, **where):
        return pltpu.make_async_remote_copy(
            src_ref=src, dst_ref=dst, send_sem=ss, recv_sem=rs, device_id=where, device_id_type=MESH
        )

    raw_copies = []
    for part in range(4):
        raw_copies.append(
            pltpu.make_async_copy(raw_hbm.at[:, pl.ds(128 * part, 128)], raw_v.at[part], local_sem.at[1 + part])
        )
        raw_copies[-1].start()
    m_copy = pltpu.make_async_copy(m_hbm, mbuf.at[yl], local_sem.at[0])
    m_copy.start()

    barrier = pltpu.get_barrier_semaphore()

    def greet_blk(t, _):
        other = lax.rem(me + t, NI)
        pl.semaphore_signal(
            barrier, inc=1, device_id={"z": other // 8, "yh": lax.rem(other // 2, YH), "co": lax.rem(other, 2)},
            device_id_type=MESH,
        )
        return 0

    lax.fori_loop(1, NI, greet_blk, 0)

    def greet_plane(t, _):
        other = lax.rem(rep + t % 8, 8)
        pl.semaphore_signal(
            barrier, inc=1,
            device_id={"yh": lax.rem(yh + t // 8, YH), "yl": other // X, "x": lax.rem(other, X)},
            device_id_type=MESH,
        )
        return 0

    for block in range(YH):
        lax.fori_loop(8 * block + 1, 8 * block + 8, greet_plane, 0)

    esend[...] = jnp.full((8, 128), occ_ref[0, 0], F32)

    c_high, c_low = halves(c_ref[...])
    for copy in raw_copies:
        copy.wait()
    total = jnp.zeros((4 * NI, 128), F32)
    for k in range(4):
        place = (
            lax.broadcasted_iota(jnp.int32, (NA, 128), 1) == lax.broadcasted_iota(jnp.int32, (NA, 128), 0) + NA * k
        ).astype(F32).astype(BF16)
        right = (mm(c_high, place).astype(BF16), mm(c_low, place).astype(BF16))
        rows = strided(raw_v, 4, k)
        total = total + mm3(halves(rows), right)
    for p in range(4):
        hsend[:, p, :] = total[NI * p : NI * (p + 1)]

    pl.semaphore_wait(barrier, NI - 1 + 28)

    def send_half(t, _):
        other = lax.rem(me + t, NI)
        remote(
            hsend.at[other], hx.at[x, me], a2a_send, a2a_recv,
            z=other // 8, yh=lax.rem(other // 2, YH), co=lax.rem(other, 2),
        ).start()
        return 0

    lax.fori_loop(1, NI, send_half, 0)
    hx[x, me] = hsend[me]

    y = yh * YL + yl
    metric = []
    for side, to in ((0, lax.rem(y + 1, 8)), (1, lax.rem(y + 7, 8))):
        rows_of = pl.ds(side * 512, 512)
        copy = remote(
            m_hbm.at[rows_of], mbuf.at[yl, rows_of], m_send.at[side], m_recv.at[side],
            yh=to // YL, yl=lax.rem(to, YL),
        )
        copy.start()
        metric.append(copy)

    distance = pick(rep, DISTANCE)
    ahead = chip + distance
    energies = []
    for core in range(CO):
        energies.append((
            jnp.logical_not(is_root),
            remote(
                esend, ebuf.at[co], e_send.at[core], e_recv.at[co],
                z=lax.rem(ahead // YH, Z), yh=lax.rem(ahead, YH), co=jnp.int32(core),
            ),
        ))
    energies.append((
        jnp.logical_and(is_root, co == 1),
        remote(esend, ebuf.at[1], e_send.at[0], e_recv.at[1], z=lax.rem(z + 2, Z), co=jnp.int32(0)),
    ))
    energies.append((
        jnp.logical_and(is_root, co == 0),
        remote(esend, ebuf.at[0], e_send.at[0], e_recv.at[0], co=jnp.int32(1)),
    ))
    for when, copy in energies:
        @pl.when(when)
        def _(copy=copy):
            copy.start()

    @pl.when(is_root)
    def _():
        ebuf[co] = esend[...]

    remote(
        hx.at[x, pl.ds(0, NI - 1)], hx.at[x, pl.ds(0, NI - 1)], a2a_send, a2a_recv, co=1 - co
    ).wait_recv()
    gathers = []
    for step in (2, 1, 3):
        copy = remote(hx.at[x], hx.at[x], x_send.at[step], x_recv.at[x], x=lax.rem(x + step, X))
        copy.start()
        gathers.append(copy)
    m_copy.wait()
    for copy in metric:
        copy.wait_recv()
    for step in (1, 3, 2):
        origin = lax.rem(x + step, X)
        remote(hx.at[origin], hx.at[origin], x_send.at[step], x_recv.at[origin], x=origin).wait_recv()

    turned = []
    for xx in range(X):
        block = jnp.concatenate([hx[xx, :, p, :] for p in range(4)], axis=0)
        turned.append(block.T)
    part = jnp.zeros((128, 256), F32)
    for k in range(4):
        left = jnp.concatenate([t[NA * k : NA * (k + 1), :] for t in turned], axis=0)
        right = strided(mbuf, 2, k)
        part = part + mm3(halves(left), halves(right))
    my_rows = pl.ds(pl.multiple_of(yl * 128, 128), 128)
    sbuf[0] = part
    fbuf[0, x, my_rows, :] = part

    up = lax.rem(z + 1, Z)
    sends = []

    def launch(copy, when=None):
        sends.append((copy, when))
        if when is None:
            copy.start()
        else:
            @pl.when(when)
            def _():
                copy.start()

    def to_holder(slot, index, steps, holder, when=None):
        launch(
            remote(
                sbuf.at[slot], fbuf.at[1 + co, x, my_rows], p_send.at[index], f_recv.at[1, rep],
                yh=lax.rem(yh + steps, YH), yl=holder // X, x=lax.rem(holder, X),
            ),
            when,
        )

    launch(remote(sbuf.at[0], sbuf.at[1], s_send.at[0], s_recv.at[0], z=up))
    for step in range(1, 4):
        to_holder(0, step - 1, step, jnp.int32(HOLDER[step]), yh + step < YH)
    for step in (6, 2, 5, 7, 3, 1, 4):
        other = lax.rem(rep + step, 8)
        launch(
            remote(
                fbuf.at[0, x, my_rows], fbuf.at[0, x, my_rows], f_send.at[step], f_recv.at[0, rep],
                yl=other // X, x=lax.rem(other, X),
            )
        )

    remote(sbuf.at[1], sbuf.at[1], s_send.at[0], s_recv.at[0], z=up).wait_recv()
    launch(remote(sbuf.at[1], sbuf.at[2], s_send.at[1], s_recv.at[1], z=up))
    for step in (2, 1, 3):
        holder = jnp.where(yh + step >= YH, HOLDER[step], HOLDER[step + 4])
        to_holder(1, 3 + step, step, holder)
    to_holder(1, 3, 0, jnp.int32(HOLDER[4]), rep != HOLDER[4])

    @pl.when(rep == HOLDER[4])
    def _():
        fbuf[1 + co, x, my_rows, :] = sbuf[1]

    remote(sbuf.at[2], sbuf.at[2], s_send.at[1], s_recv.at[1], z=up).wait_recv()
    for step in (2, 1, 3):
        to_holder(2, 7 + step, step, jnp.int32(HOLDER[step + 4]), yh + step >= YH)
    to_holder(2, 7, 0, jnp.int32(HOLDER[0]), jnp.logical_and(co == 1, jnp.logical_not(is_root)))

    @pl.when(jnp.logical_and(is_root, co == 1))
    def _():
        fbuf[2, x, my_rows, :] = sbuf[2]

    own_first = jnp.logical_and(is_root, co == 0)
    kind = jnp.where(own_first, 0, 1)
    source = jnp.where(own_first, 0, 1 + co)
    here = jnp.logical_or(is_root, rep == HOLDER[4])

    def block_of(slot, origin):
        return fbuf.at[slot, lax.rem(origin, X), pl.ds(pl.multiple_of(origin // X * 128, 128), 128)]

    def pass_on(t, _):
        origin = lax.rem(rep + t, 8)

        @pl.when(jnp.logical_not(jnp.logical_and(origin == rep, here)))
        def _():
            remote(
                block_of(source, origin), block_of(source, origin), f_send.at[0], f_recv.at[kind, origin],
                co=1 - co,
            ).wait_recv()

        remote(
            block_of(source, origin), block_of(1 + co, origin), d_send.at[origin], d_recv.at[origin], co=1 - co
        ).start()
        return 0

    lax.fori_loop(0, 8, pass_on, 0)

    def own_arrived(t, _):
        origin = lax.rem(rep + t, 8)
        remote(
            block_of(0, origin), block_of(0, origin), f_send.at[0], f_recv.at[0, origin], co=1 - co
        ).wait_recv()
        return 0

    @pl.when(jnp.logical_not(own_first))
    def _():
        lax.fori_loop(1, 8, own_arrived, 0)

    for core in range(CO):
        expected = jnp.logical_or(jnp.logical_not(is_root), co != core)

        @pl.when(expected)
        def _(core=core):
            remote(esend, ebuf.at[core], e_send.at[0], e_recv.at[core], co=1 - co).wait_recv()

    row = jnp.broadcast_to(virt_ref[...], (256, 256))
    spread = row + row.T - occ_ref[0, 0]

    def pair(order):
        which = co if order == 0 else 1 - co
        slot = jnp.where(jnp.logical_and(is_root, co == which), 0, 1 + which)
        coulomb = jnp.zeros((256, 256), F32)
        for xx in range(X):
            ih, il = halves(fbuf[0, xx])
            jh, jl = halves(fbuf[slot, xx])
            jhi[order, xx] = jh
            jlo[order, xx] = jl
            coulomb = coulomb + (mm_nt(ih, jh) + (mm_nt(ih, jl) + mm_nt(il, jh)))
        amplitude = (2.0 * coulomb - coulomb.T) / (spread - ebuf[which][0:1, 0:1])
        th, tl = halves(amplitude)
        thi[order] = th
        tlo[order] = tl

    pair(0)

    def twin_arrived(t, _):
        remote(
            block_of(2 - co, t), block_of(2 - co, t), d_send.at[t], d_recv.at[t], co=1 - co
        ).wait_recv()
        return 0

    lax.fori_loop(0, 8, twin_arrived, 0)
    pair(1)

    for step in (2, 1, 3, 0):
        xx = lax.rem(x + step, X)
        block = jnp.zeros((256, 256), F32)
        for order in range(2):
            block = block + mm3((thi[order], tlo[order]), (jhi[order, xx], jlo[order, xx]))
        for half in range(YL):
            g[xx, half] = block[:, half * NQ : (half + 1) * NQ]
        if step:
            for half in range(YL):
                launch(
                    remote(
                        g.at[xx, half], grecv.at[rep], g_send.at[YL * step + half], g_recv.at[rep],
                        yl=jnp.int32(half), x=xx,
                    )
                )
        else:
            launch(
                remote(g.at[xx, 1 - yl], grecv.at[rep], g_send.at[0], g_recv.at[rep], yl=1 - yl, x=xx)
            )
            grecv[rep] = g[xx, yl]

    def gradient_arrived(t, _):
        origin = lax.rem(rep + t, 8)
        remote(grecv.at[origin], grecv.at[origin], g_send.at[0], g_recv.at[origin], co=1 - co).wait_recv()
        return 0

    lax.fori_loop(1, 8, gradient_arrived, 0)
    result = grecv[0]
    for origin in range(1, 8):
        result = result + grecv[origin]
    out_ref[...] = result

    remote(
        hsend.at[pl.ds(0, NI - 1)], hx.at[x, pl.ds(0, NI - 1)], a2a_send, a2a_recv, co=1 - co
    ).wait_send()
    for copy in metric + gathers:
        copy.wait_send()
    for when, copy in energies:
        @pl.when(when)
        def _(copy=copy):
            copy.wait_send()
    for copy, when in sends:
        if when is None:
            copy.wait_send()
        else:
            @pl.when(when)
            def _(copy=copy):
                copy.wait_send()

    def passed(t, _):
        remote(
            block_of(source, t), block_of(1 + co, t), d_send.at[t], d_recv.at[t], co=1 - co
        ).wait_send()
        return 0

    lax.fori_loop(0, 8, passed, 0)


def per_device(raw_integrals, virtual_coeffs, metric_root, occ_energies, virt_energies):
    vmem = pl.BlockSpec(memory_space=pltpu.VMEM)
    anywhere = pl.BlockSpec(memory_space=pl.ANY)
    dma = pltpu.SemaphoreType.DMA
    out = pl.pallas_call(
        kernel,
        out_shape=jax.ShapeDtypeStruct((256, NQ), F32),
        in_specs=[anywhere, vmem, anywhere, pl.BlockSpec(memory_space=pltpu.SMEM), vmem],
        out_specs=vmem,
        scratch_shapes=[
            pltpu.VMEM((4, NI * NP, 128), F32),
            pltpu.VMEM((YL, 1024, NQ), F32),
            pltpu.VMEM((NI, 4, 128), F32),
            pltpu.VMEM((X, NI, 4, 128), F32),
            pltpu.VMEM((3, 128, 256), F32),
            pltpu.VMEM((3, X, 256, 256), F32),
            pltpu.VMEM((2, X, 256, 256), BF16),
            pltpu.VMEM((2, X, 256, 256), BF16),
            pltpu.VMEM((2, 256, 256), BF16),
            pltpu.VMEM((2, 256, 256), BF16),
            pltpu.VMEM((8, 128), F32),
            pltpu.VMEM((2, 8, 128), F32),
            pltpu.VMEM((X, YL, 256, NQ), F32),
            pltpu.VMEM((8, 256, NQ), F32),
            dma((5,)), dma, dma, dma((2,)), dma((2,)), dma((2,)), dma((2,)), dma((4,)), dma((4,)),
            dma((2,)), dma((2,)), dma((8,)), dma((2, 8)), dma((11,)), dma((8,)), dma((8,)), dma((8,)), dma((8,)),
        ],
        compiler_params=pltpu.CompilerParams(
            collective_id=0, has_side_effects=True, vmem_limit_bytes=48 * 1024 * 1024
        ),
        name="gradient_density",
    )(
        raw_integrals.reshape(NI * NP, NM), virtual_coeffs, metric_root,
        occ_energies.reshape(1, 1), virt_energies.reshape(1, 256),
    )
    return out[None]


def solution(mesh):
    finer = Mesh(mesh.devices.reshape(Z, YH, CO, YL, X), BLK + REP)
    return jax.shard_map(
        per_device,
        mesh=finer,
        in_specs=(P(None, BLK, None), P(None, REP), P(None, REP), P(BLK), P()),
        out_specs=P(BLK, None, REP),
        check_vma=False,
    )
```

time: 295 us -> 97.3 us (0.33)
  the two profiles are of different devices: /device:TPU:1 before, /device:TPU:13 now
where the time goes in v1:
time: 97.3 us; the launch traced here: 97 us
  Pallas kernels  91.4 us (94%)
  local copies, waits for them, and re-layouts  4.93 us (5%)
    pallas_call x1, Pallas kernels, per_device(): pl.pallas_call(kernel, out_shape=jax.ShapeDtypeStruct((256, NQ), F32), in...  91.4 us
    unnamed x8, local copies, waits for them, and re-layouts  4.93 us

profile of v1, /device:TPU:13, one launch (start us, length us, event | category | flops | bytes accessed | tf_op | source)
XLA Modules:
  0.0 97.0 jit_solution(6325534960943616200)
XLA Ops:
  0.7 1.0 copy.6.c_ref
  1.6 0.0 copy-start
  1.6 1.6 %copy-done = f32[64,16,512]{2,1,0:T(8,128)S(1)} copy-done((f32[64,16,512]{2,1,0:T(8,128)S(1)}, f32[64,16,512]{2,1,0:T(8,128)}, u32[]{:S(2)}) %copy-start) | copy-done | bytes 2097176
  3.2 0.0 copy-start.1
  3.2 1.0 %copy-done.1 = f32[1024,128]{1,0:T(8,128)S(1)} copy-done((f32[1024,128]{1,0:T(8,128)S(1)}, f32[1024,128]{1,0:T(8,128)}, u32[]{:S(2)}) %copy-start.1) | copy-done | bytes 524312
  4.3 0.0 copy-start.2
  4.3 0.7 copy-done.2
  4.9 91.4 %gradient_density.1 = f32[256,128]{1,0:T(8,128)S(1)} custom-call(f32[1024,512]{1,0:T(8,128)S(1)} %bitcast.5, f32[512,32]{1,0:T(8,128)S(1)} %copy.6.c_ref, f32[1024,128]{1,0:T(8,128)S(1)} %copy-done.1, f32[1,1]{1,0:T(1,128)} %bitcast.4.occ_ref, f32[1,256]{1,0:T(1,128)S(1)} %bitcast.7), custom_call_target="tpu_custom_call" | custom-call | tf_op jit(solution)/shard_map/gradient_density/pallas_call | solution.py:386
  96.4 0.7 copy.9
Async XLA Ops:
  1.6 1.6 %copy-start = (f32[64,16,512]{2,1,0:T(8,128)S(1)}, f32[64,16,512]{2,1,0:T(8,128)}, u32[]{:S(2)}) copy-start(f32[64,16,512]{2,1,0:T(8,128)} %param.5) | copy-start | bytes 6291460
  3.2 1.0 %copy-start.1 = (f32[1024,128]{1,0:T(8,128)S(1)}, f32[1024,128]{1,0:T(8,128)}, u32[]{:S(2)}) copy-start(f32[1024,128]{1,0:T(8,128)} %m_hbm.1) | copy-start | bytes 1572868
  4.3 0.7 copy-start.2

commit v2 on v1

--- a/solution.py
+++ b/solution.py
@@ -50,8 +50,8 @@
 
 
 def kernel(
-    raw_hbm, c_ref, m_hbm, occ_ref, virt_ref, out_ref,
-    raw_v, mbuf, hsend, hx, sbuf, fbuf, jhi, jlo, thi, tlo, esend, ebuf, g, grecv,
+    raw_hbm, c_hbm, m_hbm, occ_ref, virt_hbm, out_ref,
+    raw_v, c_v, virt_v, mbuf, hsend, hx, sbuf, fbuf, jhi, jlo, thi, tlo, esend, ebuf, g, grecv,
     local_sem, a2a_send, a2a_recv, m_send, m_recv, e_send, e_recv, x_send, x_recv,
     s_send, s_recv, f_send, f_recv, p_send, d_send, d_recv, g_send, g_recv,
 ):
@@ -67,6 +67,8 @@
             src_ref=src, dst_ref=dst, send_sem=ss, recv_sem=rs, device_id=where, device_id_type=MESH
         )
 
+    c_copy = pltpu.make_async_copy(c_hbm, c_v, local_sem.at[5])
+    c_copy.start()
     raw_copies = []
     for part in range(4):
         raw_copies.append(
@@ -75,34 +77,31 @@
         raw_copies[-1].start()
     m_copy = pltpu.make_async_copy(m_hbm, mbuf.at[yl], local_sem.at[0])
     m_copy.start()
+    virt_copy = pltpu.make_async_copy(virt_hbm, virt_v, local_sem.at[6])
+    virt_copy.start()
+
+    zs = [lax.rem(z + step, Z) for step in range(Z)]
+    yhs = [lax.rem(yh + step, YH) for step in range(YH)]
+    cos = [co, 1 - co]
+    yls = [yl, 1 - yl]
+    xs = [lax.rem(x + step, X) for step in range(X)]
+    across_blk = [(a, b, c) for a in (4, 3, 5, 2, 6, 1, 7, 0) for b in (2, 1, 3, 0) for c in (0, 1)][:-2] + [(0, 0, 1)]
+    across_plane = [(a, b, c) for a in (2, 1, 3, 0) for b in (0, 1) for c in (2, 1, 3, 0) if (b, c) != (0, 0)]
 
     barrier = pltpu.get_barrier_semaphore()
-
-    def greet_blk(t, _):
-        other = lax.rem(me + t, NI)
+    for a, b, c in across_blk:
         pl.semaphore_signal(
-            barrier, inc=1, device_id={"z": other // 8, "yh": lax.rem(other // 2, YH), "co": lax.rem(other, 2)},
-            device_id_type=MESH,
-        )
-        return 0
-
-    lax.fori_loop(1, NI, greet_blk, 0)
-
-    def greet_plane(t, _):
-        other = lax.rem(rep + t % 8, 8)
+            barrier, inc=1, device_id={"z": zs[a], "yh": yhs[b], "co": cos[c]}, device_id_type=MESH
+        )
+    for a, b, c in across_plane:
         pl.semaphore_signal(
-            barrier, inc=1,
-            device_id={"yh": lax.rem(yh + t // 8, YH), "yl": other // X, "x": lax.rem(other, X)},
-            device_id_type=MESH,
-        )
-        return 0
-
-    for block in range(YH):
-        lax.fori_loop(8 * block + 1, 8 * block + 8, greet_plane, 0)
-
-    esend[...] = jnp.full((8, 128), occ_ref[0, 0], F32)
-
-    c_high, c_low = halves(c_ref[...])
+            barrier, inc=1, device_id={"yh": yhs[a], "yl": yls[b], "x": xs[c]}, device_id_type=MESH
+        )
+
+    esend[...] = jnp.full((8, 128), occ_ref[0], F32)
+
+    c_copy.wait()
+    c_high, c_low = halves(c_v[...].T)
     for copy in raw_copies:
         copy.wait()
     total = jnp.zeros((4 * NI, 128), F32)
@@ -116,17 +115,11 @@
     for p in range(4):
         hsend[:, p, :] = total[NI * p : NI * (p + 1)]
 
-    pl.semaphore_wait(barrier, NI - 1 + 28)
-
-    def send_half(t, _):
-        other = lax.rem(me + t, NI)
-        remote(
-            hsend.at[other], hx.at[x, me], a2a_send, a2a_recv,
-            z=other // 8, yh=lax.rem(other // 2, YH), co=lax.rem(other, 2),
-        ).start()
-        return 0
-
-    lax.fori_loop(1, NI, send_half, 0)
+    pl.semaphore_wait(barrier, len(across_blk) + len(across_plane))
+
+    for a, b, c in across_blk:
+        other = (zs[a] * YH + yhs[b]) * CO + cos[c]
+        remote(hsend.at[other], hx.at[x, me], a2a_send, a2a_recv, z=zs[a], yh=yhs[b], co=cos[c]).start()
     hx[x, me] = hsend[me]
 
     y = yh * YL + yl
@@ -220,12 +213,27 @@
     launch(remote(sbuf.at[0], sbuf.at[1], s_send.at[0], s_recv.at[0], z=up))
     for step in range(1, 4):
         to_holder(0, step - 1, step, jnp.int32(HOLDER[step]), yh + step < YH)
-    for step in (6, 2, 5, 7, 3, 1, 4):
-        other = lax.rem(rep + step, 8)
+    other_rows = pl.ds(pl.multiple_of((1 - yl) * 128, 128), 128)
+    twin = (1 - yl) * X + x
+    launch(
+        remote(
+            fbuf.at[0, x, my_rows], fbuf.at[0, x, my_rows], f_send.at[0], f_recv.at[0, rep], yl=1 - yl
+        )
+    )
+    for step in (2, 1, 3):
         launch(
             remote(
-                fbuf.at[0, x, my_rows], fbuf.at[0, x, my_rows], f_send.at[step], f_recv.at[0, rep],
-                yl=other // X, x=lax.rem(other, X),
+                fbuf.at[0, x, my_rows], fbuf.at[0, x, my_rows], f_send.at[step], f_recv.at[0, rep], x=xs[step]
+            )
+        )
+    remote(
+        fbuf.at[0, x, other_rows], fbuf.at[0, x, other_rows], f_send.at[0], f_recv.at[0, twin], co=1 - co
+    ).wait_recv()
+    for step in (2, 1, 3):
+        launch(
+            remote(
+                fbuf.at[0, x, other_rows], fbuf.at[0, x, other_rows], f_send.at[4 + step], f_recv.at[0, twin],
+                x=xs[step],
             )
         )
 
@@ -260,7 +268,9 @@
     def pass_on(t, _):
         origin = lax.rem(rep + t, 8)
 
-        @pl.when(jnp.logical_not(jnp.logical_and(origin == rep, here)))
+        known = jnp.logical_or(jnp.logical_and(origin == rep, here), jnp.logical_and(origin == twin, own_first))
+
+        @pl.when(jnp.logical_not(known))
         def _():
             remote(
                 block_of(source, origin), block_of(source, origin), f_send.at[0], f_recv.at[kind, origin],
@@ -276,9 +286,13 @@
 
     def own_arrived(t, _):
         origin = lax.rem(rep + t, 8)
-        remote(
-            block_of(0, origin), block_of(0, origin), f_send.at[0], f_recv.at[0, origin], co=1 - co
-        ).wait_recv()
+
+        @pl.when(origin != twin)
+        def _():
+            remote(
+                block_of(0, origin), block_of(0, origin), f_send.at[0], f_recv.at[0, origin], co=1 - co
+            ).wait_recv()
+
         return 0
 
     @pl.when(jnp.logical_not(own_first))
@@ -292,8 +306,9 @@
         def _(core=core):
             remote(esend, ebuf.at[core], e_send.at[0], e_recv.at[core], co=1 - co).wait_recv()
 
-    row = jnp.broadcast_to(virt_ref[...], (256, 256))
-    spread = row + row.T - occ_ref[0, 0]
+    virt_copy.wait()
+    row = jnp.broadcast_to(virt_v[...], (256, 256))
+    spread = row + row.T - occ_ref[0]
 
     def pair(order):
         which = co if order == 0 else 1 - co
@@ -386,10 +401,12 @@
     out = pl.pallas_call(
         kernel,
         out_shape=jax.ShapeDtypeStruct((256, NQ), F32),
-        in_specs=[anywhere, vmem, anywhere, pl.BlockSpec(memory_space=pltpu.SMEM), vmem],
+        in_specs=[anywhere, anywhere, anywhere, pl.BlockSpec(memory_space=pltpu.SMEM), anywhere],
         out_specs=vmem,
         scratch_shapes=[
             pltpu.VMEM((4, NI * NP, 128), F32),
+            pltpu.VMEM((NA, NM), F32),
+            pltpu.VMEM((1, 256), F32),
             pltpu.VMEM((YL, 1024, NQ), F32),
             pltpu.VMEM((NI, 4, 128), F32),
             pltpu.VMEM((X, NI, 4, 128), F32),
@@ -403,16 +420,16 @@
             pltpu.VMEM((2, 8, 128), F32),
             pltpu.VMEM((X, YL, 256, NQ), F32),
             pltpu.VMEM((8, 256, NQ), F32),
-            dma((5,)), dma, dma, dma((2,)), dma((2,)), dma((2,)), dma((2,)), dma((4,)), dma((4,)),
+            dma((7,)), dma, dma, dma((2,)), dma((2,)), dma((2,)), dma((2,)), dma((4,)), dma((4,)),
             dma((2,)), dma((2,)), dma((8,)), dma((2, 8)), dma((11,)), dma((8,)), dma((8,)), dma((8,)), dma((8,)),
         ],
         compiler_params=pltpu.CompilerParams(
-            collective_id=0, has_side_effects=True, vmem_limit_bytes=48 * 1024 * 1024
+            collective_id=0, has_side_effects=True, vmem_limit_bytes=67043328
         ),
         name="gradient_density",
     )(
-        raw_integrals.reshape(NI * NP, NM), virtual_coeffs, metric_root,
-        occ_energies.reshape(1, 1), virt_energies.reshape(1, 256),
+        raw_integrals.reshape(NI * NP, NM), virtual_coeffs.T, metric_root,
+        occ_energies, virt_energies.reshape(1, 256),
     )
     return out[None]
 

time: 97.3 us -> 93.5 us (0.961)
  the two profiles are of different devices: /device:TPU:13 before, /device:TPU:4 now
where the time goes in v2:
time: 93.5 us; the launch traced here: 93.3 us
  Pallas kernels  91.1 us (97%)
  local copies, waits for them, and re-layouts  1.57 us (2%)
    pallas_call x1, Pallas kernels, per_device(): pl.pallas_call(kernel, out_shape=jax.ShapeDtypeStruct((256, NQ), F32), in...  91.1 us

profile of v2, /device:TPU:4, one launch (start us, length us, event | category | flops | bytes accessed | tf_op | source)
XLA Modules:
  0.0 93.3 jit_solution(12629839736371825749)
XLA Ops:
  0.7 91.1 %gradient_density.1 = f32[256,128]{1,0:T(8,128)} custom-call(f32[1024,512]{1,0:T(8,128)} %bitcast.4, f32[32,512]{1,0:T(8,128)} %bitcast.6, f32[1024,128]{1,0:T(8,128)} %m_hbm.1, f32[1]{0:T(128)S(6)} %copy.7.occ_ref, f32[1,256]{1,0:T(1,128)} %bitcast.7), custom_call_target="tpu_custom_call" | custom-call | tf_op jit(solution)/shard_map/gradient_density/pallas_call | solution.py:401
  91.8 1.6 %copy.8 = f32[1,256,128]{2,1,0:T(8,128)} copy(f32[1,256,128]{2,1,0:T(8,128)} %bitcast.5) | data formatting | bytes 262144

commit v3 on v2

--- a/solution.py
+++ b/solution.py
@@ -13,8 +13,8 @@
 BLK = ("z", "yh", "co")
 REP = ("yl", "x")
 NI, NP, NM, NA, NQ = 64, 16, 512, 32, 128
-HOLDER = (0, 1, 3, 4, 6, 2, 7, 5)
-DISTANCE = (0, 1, 5, 2, 3, 7, 4, 6)
+HOLDER = (1, 2, 0, 6, 4, 3, 5, 7)
+DISTANCE = (2, 0, 1, 5, 4, 6, 3, 7)
 
 
 def halves(v):

time: 93.5 us -> 88 us (0.941)
  the two profiles are of different devices: /device:TPU:4 before, /device:TPU:1 now
where the time goes in v3:
time: 88 us; the launch traced here: 87.8 us
  Pallas kernels  85.6 us (97%)
  local copies, waits for them, and re-layouts  1.57 us (2%)
    pallas_call x1, Pallas kernels, per_device(): pl.pallas_call(kernel, out_shape=jax.ShapeDtypeStruct((256, NQ), F32), in...  85.6 us

profile of v3, /device:TPU:1, one launch (start us, length us, event | category | flops | bytes accessed | tf_op | source)
XLA Modules:
  0.0 87.8 jit_solution(6165345950119546988)
XLA Ops:
  0.7 85.6 %gradient_density.1 = f32[256,128]{1,0:T(8,128)} custom-call(f32[1024,512]{1,0:T(8,128)} %bitcast.4, f32[32,512]{1,0:T(8,128)} %bitcast.6, f32[1024,128]{1,0:T(8,128)} %m_hbm.1, f32[1]{0:T(128)S(6)} %copy.7.occ_ref, f32[1,256]{1,0:T(1,128)} %bitcast.7), custom_call_target="tpu_custom_call" | custom-call | tf_op jit(solution)/shard_map/gradient_density/pallas_call | solution.py:401
  86.3 1.6 %copy.8 = f32[1,256,128]{2,1,0:T(8,128)} copy(f32[1,256,128]{2,1,0:T(8,128)} %bitcast.5) | data formatting | bytes 262144

commit v4 on v3

--- a/solution.py
+++ b/solution.py
@@ -13,8 +13,7 @@
 BLK = ("z", "yh", "co")
 REP = ("yl", "x")
 NI, NP, NM, NA, NQ = 64, 16, 512, 32, 128
-HOLDER = (1, 2, 0, 6, 4, 3, 5, 7)
-DISTANCE = (2, 0, 1, 5, 4, 6, 3, 7)
+DISTANCE = (1, 5, 2, 0, 3, 7, 6, 4)
 
 
 def halves(v):
@@ -51,16 +50,16 @@
 
 def kernel(
     raw_hbm, c_hbm, m_hbm, occ_ref, virt_hbm, out_ref,
-    raw_v, c_v, virt_v, mbuf, hsend, hx, sbuf, fbuf, jhi, jlo, thi, tlo, esend, ebuf, g, grecv,
+    raw_v, c_v, virt_v, mbuf, hsend, hx, sbuf, rbuf, fbuf, jhi, jlo, thi, tlo, esend, ebuf, g, grecv,
     local_sem, a2a_send, a2a_recv, m_send, m_recv, e_send, e_recv, x_send, x_recv,
-    s_send, s_recv, f_send, f_recv, p_send, d_send, d_recv, g_send, g_recv,
+    s_send, s_recv, f_send, f_recv, p_send, r_recv, c_send, q_send, d_send, d_recv, g_send, g_recv,
 ):
     z, yh, co = lax.axis_index("z"), lax.axis_index("yh"), lax.axis_index("co")
     yl, x = lax.axis_index("yl"), lax.axis_index("x")
     me = (z * YH + yh) * CO + co
     chip = z * YH + yh
     rep = yl * X + x
-    is_root = rep == HOLDER[0]
+    is_root = jnp.logical_and(yl == 0, x == 3)
 
     def remote(src, dst, ss, rs, **where):
         return pltpu.make_async_remote_copy(
@@ -189,7 +188,7 @@
     sbuf[0] = part
     fbuf[0, x, my_rows, :] = part
 
-    up = lax.rem(z + 1, Z)
+    up = zs[1]
     sends = []
 
     def launch(copy, when=None):
@@ -201,66 +200,95 @@
             def _():
                 copy.start()
 
-    def to_holder(slot, index, steps, holder, when=None):
+    wraps = {1: yh == YH - 1, 3: yh > 0}
+
+    def to_edge(slot, index, step, k, when=None):
         launch(
             remote(
-                sbuf.at[slot], fbuf.at[1 + co, x, my_rows], p_send.at[index], f_recv.at[1, rep],
-                yh=lax.rem(yh + steps, YH), yl=holder // X, x=lax.rem(holder, X),
+                sbuf.at[slot], rbuf.at[k, yl], p_send.at[index], r_recv.at[k, yl],
+                yh=yhs[step], yl=jnp.int32(step // 2),
             ),
             when,
         )
 
-    launch(remote(sbuf.at[0], sbuf.at[1], s_send.at[0], s_recv.at[0], z=up))
-    for step in range(1, 4):
-        to_holder(0, step - 1, step, jnp.int32(HOLDER[step]), yh + step < YH)
+    def gather_row(origin_rows, origin, index):
+        for step in (2, 1, 3):
+            launch(
+                remote(
+                    fbuf.at[0, x, origin_rows], fbuf.at[0, x, origin_rows], f_send.at[index + step],
+                    f_recv.at[0, origin], x=xs[step],
+                )
+            )
+
     other_rows = pl.ds(pl.multiple_of((1 - yl) * 128, 128), 128)
     twin = (1 - yl) * X + x
-    launch(
-        remote(
-            fbuf.at[0, x, my_rows], fbuf.at[0, x, my_rows], f_send.at[0], f_recv.at[0, rep], yl=1 - yl
-        )
-    )
-    for step in (2, 1, 3):
-        launch(
-            remote(
-                fbuf.at[0, x, my_rows], fbuf.at[0, x, my_rows], f_send.at[step], f_recv.at[0, rep], x=xs[step]
-            )
-        )
+    launch(remote(sbuf.at[0], sbuf.at[1], s_send.at[0], s_recv.at[0], z=up))
+    launch(remote(sbuf.at[0], fbuf.at[0, x, my_rows], f_send.at[0], f_recv.at[0, rep], yl=1 - yl))
+    for step in (1, 3):
+        to_edge(0, step // 2, step, 0, jnp.logical_not(wraps[step]))
+    gather_row(my_rows, rep, 0)
     remote(
         fbuf.at[0, x, other_rows], fbuf.at[0, x, other_rows], f_send.at[0], f_recv.at[0, twin], co=1 - co
     ).wait_recv()
-    for step in (2, 1, 3):
+    gather_row(other_rows, twin, 4)
+
+    remote(sbuf.at[1], sbuf.at[1], s_send.at[0], s_recv.at[0], z=up).wait_recv()
+    launch(remote(sbuf.at[1], sbuf.at[2], s_send.at[1], s_recv.at[1], z=up))
+    for step in (1, 3):
+        to_edge(1, 2 + step // 2, step, jnp.where(wraps[step], 0, 1))
+    launch(remote(sbuf.at[1], rbuf.at[3, 0], p_send.at[6], r_recv.at[3, 0], yl=jnp.int32(1)), yl == 0)
+
+    goes_on = jnp.where(yl == 0, jnp.where(yh == YH - 1, 1, 0), jnp.where(yh == 0, 0, 1))
+    onward = jnp.where(yl == 0, yhs[1], yhs[3])
+
+    def deliver(src, k, row, when=None):
+        rows = pl.ds(row * 128, 128) if isinstance(row, int) else pl.ds(pl.multiple_of(row * 128, 128), 128)
+        away = x != k if when is None else jnp.logical_and(x != k, when)
         launch(
             remote(
-                fbuf.at[0, x, other_rows], fbuf.at[0, x, other_rows], f_send.at[4 + step], f_recv.at[0, twin],
-                x=xs[step],
-            )
-        )
-
-    remote(sbuf.at[1], sbuf.at[1], s_send.at[0], s_recv.at[0], z=up).wait_recv()
-    launch(remote(sbuf.at[1], sbuf.at[2], s_send.at[1], s_recv.at[1], z=up))
-    for step in (2, 1, 3):
-        holder = jnp.where(yh + step >= YH, HOLDER[step], HOLDER[step + 4])
-        to_holder(1, 3 + step, step, holder)
-    to_holder(1, 3, 0, jnp.int32(HOLDER[4]), rep != HOLDER[4])
-
-    @pl.when(rep == HOLDER[4])
+                src, fbuf.at[1 + co, x, rows], q_send.at[k, row], f_recv.at[1, row * X + x], x=jnp.int32(k)
+            ),
+            away,
+        )
+
+        @pl.when(x == k if when is None else jnp.logical_and(x == k, when))
+        def _():
+            fbuf[1 + co, x, rows, :] = src[...]
+
+    def arrived(k, row):
+        return remote(rbuf.at[k, row], rbuf.at[k, row], q_send.at[0, 0], r_recv.at[k, row], co=1 - co)
+
+    def relay(k):
+        for row in range(YL):
+            arrived(k, row).wait_recv()
+            if k < 2:
+                launch(
+                    remote(rbuf.at[k, row], rbuf.at[2, row], c_send.at[k, row], r_recv.at[2, row], yh=onward),
+                    goes_on == k,
+                )
+            deliver(rbuf.at[k, row], k, row)
+
+    relay(0)
+    remote(sbuf.at[2], sbuf.at[2], s_send.at[1], s_recv.at[1], z=up).wait_recv()
+    for step in (1, 3):
+        to_edge(2, 4 + step // 2, step, 1, wraps[step])
+    last = jnp.logical_and(yl == 1, co == 1)
+    launch(remote(sbuf.at[2], rbuf.at[3, 1], p_send.at[7], r_recv.at[3, 1], yl=jnp.int32(0)), last)
+    relay(1)
+
+    takes = jnp.logical_or(yl == 1, co == 1)
+
+    @pl.when(takes)
     def _():
-        fbuf[1 + co, x, my_rows, :] = sbuf[1]
-
-    remote(sbuf.at[2], sbuf.at[2], s_send.at[1], s_recv.at[1], z=up).wait_recv()
-    for step in (2, 1, 3):
-        to_holder(2, 7 + step, step, jnp.int32(HOLDER[step + 4]), yh + step >= YH)
-    to_holder(2, 7, 0, jnp.int32(HOLDER[0]), jnp.logical_and(co == 1, jnp.logical_not(is_root)))
-
-    @pl.when(jnp.logical_and(is_root, co == 1))
-    def _():
-        fbuf[2, x, my_rows, :] = sbuf[2]
+        arrived(3, 1 - yl).wait_recv()
+
+    deliver(rbuf.at[3, 1 - yl], 3, 1 - yl, takes)
+    deliver(sbuf.at[2 - yl], 3, yl, takes)
+    relay(2)
 
     own_first = jnp.logical_and(is_root, co == 0)
     kind = jnp.where(own_first, 0, 1)
     source = jnp.where(own_first, 0, 1 + co)
-    here = jnp.logical_or(is_root, rep == HOLDER[4])
 
     def block_of(slot, origin):
         return fbuf.at[slot, lax.rem(origin, X), pl.ds(pl.multiple_of(origin // X * 128, 128), 128)]
@@ -268,7 +296,7 @@
     def pass_on(t, _):
         origin = lax.rem(rep + t, 8)
 
-        known = jnp.logical_or(jnp.logical_and(origin == rep, here), jnp.logical_and(origin == twin, own_first))
+        known = lax.rem(origin, X) == x
 
         @pl.when(jnp.logical_not(known))
         def _():
@@ -411,6 +439,7 @@
             pltpu.VMEM((NI, 4, 128), F32),
             pltpu.VMEM((X, NI, 4, 128), F32),
             pltpu.VMEM((3, 128, 256), F32),
+            pltpu.VMEM((4, YL, 128, 256), F32),
             pltpu.VMEM((3, X, 256, 256), F32),
             pltpu.VMEM((2, X, 256, 256), BF16),
             pltpu.VMEM((2, X, 256, 256), BF16),
@@ -421,7 +450,8 @@
             pltpu.VMEM((X, YL, 256, NQ), F32),
             pltpu.VMEM((8, 256, NQ), F32),
             dma((7,)), dma, dma, dma((2,)), dma((2,)), dma((2,)), dma((2,)), dma((4,)), dma((4,)),
-            dma((2,)), dma((2,)), dma((8,)), dma((2, 8)), dma((11,)), dma((8,)), dma((8,)), dma((8,)), dma((8,)),
+            dma((2,)), dma((2,)), dma((8,)), dma((2, 8)),
+            dma((8,)), dma((4, 2)), dma((2, 2)), dma((4, 2)), dma((8,)), dma((8,)), dma((8,)), dma((8,)),
         ],
         compiler_params=pltpu.CompilerParams(
             collective_id=0, has_side_effects=True, vmem_limit_bytes=67043328

time: 88 us -> 99.4 us (1.13)
  the two profiles are of different devices: /device:TPU:1 before, /device:TPU:20 now
where the time goes in v4:
time: 99.4 us; the launch traced here: 99.2 us
  Pallas kernels  97 us (98%)
  local copies, waits for them, and re-layouts  1.57 us (2%)
    pallas_call x1, Pallas kernels, per_device(): pl.pallas_call(kernel, out_shape=jax.ShapeDtypeStruct((256, NQ), F32), in...  97 us

profile of v4, /device:TPU:20, one launch (start us, length us, event | category | flops | bytes accessed | tf_op | source)
XLA Modules:
  0.0 99.2 jit_solution(15914549552235204349)
XLA Ops:
  0.7 97.0 %gradient_density.1 = f32[256,128]{1,0:T(8,128)} custom-call(f32[1024,512]{1,0:T(8,128)} %bitcast.4, f32[32,512]{1,0:T(8,128)} %bitcast.6, f32[1024,128]{1,0:T(8,128)} %m_hbm.1, f32[1]{0:T(128)S(6)} %copy.7.occ_ref, f32[1,256]{1,0:T(1,128)} %bitcast.7), custom_call_target="tpu_custom_call" | custom-call | tf_op jit(solution)/shard_map/gradient_density/pallas_call | solution.py:429
  97.6 1.6 %copy.8 = f32[1,256,128]{2,1,0:T(8,128)} copy(f32[1,256,128]{2,1,0:T(8,128)} %bitcast.5) | data formatting | bytes 262144

commit v5 on v3

--- a/solution.py
+++ b/solution.py
@@ -51,7 +51,7 @@
 
 def kernel(
     raw_hbm, c_hbm, m_hbm, occ_ref, virt_hbm, out_ref,
-    raw_v, c_v, virt_v, mbuf, hsend, hx, sbuf, fbuf, jhi, jlo, thi, tlo, esend, ebuf, g, grecv,
+    raw_v, c_v, virt_v, mbuf, hsend, hx, sbuf, fbuf, jhi, jlo, thi, tlo, esend, ebuf, g, grecv, tbuf,
     local_sem, a2a_send, a2a_recv, m_send, m_recv, e_send, e_recv, x_send, x_recv,
     s_send, s_recv, f_send, f_recv, p_send, d_send, d_recv, g_send, g_recv,
 ):
@@ -336,37 +336,39 @@
     lax.fori_loop(0, 8, twin_arrived, 0)
     pair(1)
 
+    def to_column(step, half, index):
+        launch(
+            remote(
+                g.at[xs[step], half], grecv.at[x, half], g_send.at[step, index], g_recv.at[x, index], x=xs[step]
+            )
+        )
+
     for step in (2, 1, 3, 0):
-        xx = lax.rem(x + step, X)
+        xx = xs[step]
         block = jnp.zeros((256, 256), F32)
         for order in range(2):
             block = block + mm3((thi[order], tlo[order]), (jhi[order, xx], jlo[order, xx]))
         for half in range(YL):
             g[xx, half] = block[:, half * NQ : (half + 1) * NQ]
         if step:
-            for half in range(YL):
-                launch(
-                    remote(
-                        g.at[xx, half], grecv.at[rep], g_send.at[YL * step + half], g_recv.at[rep],
-                        yl=jnp.int32(half), x=xx,
-                    )
-                )
-        else:
-            launch(
-                remote(g.at[xx, 1 - yl], grecv.at[rep], g_send.at[0], g_recv.at[rep], yl=1 - yl, x=xx)
-            )
-            grecv[rep] = g[xx, yl]
-
-    def gradient_arrived(t, _):
-        origin = lax.rem(rep + t, 8)
-        remote(grecv.at[origin], grecv.at[origin], g_send.at[0], g_recv.at[origin], co=1 - co).wait_recv()
-        return 0
-
-    lax.fori_loop(1, 8, gradient_arrived, 0)
-    result = grecv[0]
-    for origin in range(1, 8):
-        result = result + grecv[origin]
-    out_ref[...] = result
+            to_column(step, 1 - yl, 0)
+    for step in (2, 1, 3):
+        to_column(step, yl, 1)
+
+    def column_sum(half, index):
+        for step in (1, 3, 2):
+            block = grecv.at[xs[step], half]
+            remote(block, block, g_send.at[0, 0], g_recv.at[xs[step], index], co=1 - co).wait_recv()
+        result = g[x, half]
+        for step in (1, 2, 3):
+            result = result + grecv[xs[step], half]
+        return result
+
+    tbuf[0] = column_sum(1 - yl, 0)
+    launch(remote(tbuf.at[0], tbuf.at[1], g_send.at[0, 0], g_recv.at[x, 0], yl=1 - yl))
+    result = column_sum(yl, 1)
+    remote(tbuf.at[1], tbuf.at[1], g_send.at[0, 0], g_recv.at[x, 0], co=1 - co).wait_recv()
+    out_ref[...] = result + tbuf[1]
 
     remote(
         hsend.at[pl.ds(0, NI - 1)], hx.at[x, pl.ds(0, NI - 1)], a2a_send, a2a_recv, co=1 - co
@@ -419,9 +421,10 @@
             pltpu.VMEM((8, 128), F32),
             pltpu.VMEM((2, 8, 128), F32),
             pltpu.VMEM((X, YL, 256, NQ), F32),
-            pltpu.VMEM((8, 256, NQ), F32),
+            pltpu.VMEM((X, YL, 256, NQ), F32),
+            pltpu.VMEM((2, 256, NQ), F32),
             dma((7,)), dma, dma, dma((2,)), dma((2,)), dma((2,)), dma((2,)), dma((4,)), dma((4,)),
-            dma((2,)), dma((2,)), dma((8,)), dma((2, 8)), dma((11,)), dma((8,)), dma((8,)), dma((8,)), dma((8,)),
+            dma((2,)), dma((2,)), dma((8,)), dma((2, 8)), dma((11,)), dma((8,)), dma((8,)), dma((X, 2)), dma((X, 2)),
         ],
         compiler_params=pltpu.CompilerParams(
             collective_id=0, has_side_effects=True, vmem_limit_bytes=67043328

time: 88 us -> 85.1 us (0.967)
  Pallas kernels: 85.6 us -> 82.7 us
    pallas_call x1, Pallas kernels: 85.6 us -> 82.7 us  [per_device(): pl.pallas_call(kernel, out_shape=jax.ShapeDtypeStruct((256, NQ), F32), in...]
where the time goes in v5:
time: 85.1 us; the launch traced here: 84.9 us
  Pallas kernels  82.7 us (97%)
  local copies, waits for them, and re-layouts  1.57 us (2%)
    pallas_call x1, Pallas kernels, per_device(): pl.pallas_call(kernel, out_shape=jax.ShapeDtypeStruct((256, NQ), F32), in...  82.7 us

profile of v5, /device:TPU:1, one launch (start us, length us, event | category | flops | bytes accessed | tf_op | source)
XLA Modules:
  0.0 84.9 jit_solution(15166439237904553464)
XLA Ops:
  0.7 82.7 %gradient_density.1 = f32[256,128]{1,0:T(8,128)} custom-call(f32[1024,512]{1,0:T(8,128)} %bitcast.4, f32[32,512]{1,0:T(8,128)} %bitcast.6, f32[1024,128]{1,0:T(8,128)} %m_hbm.1, f32[1]{0:T(128)S(6)} %copy.7.occ_ref, f32[1,256]{1,0:T(1,128)} %bitcast.7), custom_call_target="tpu_custom_call" | custom-call | tf_op jit(solution)/shard_map/gradient_density/pallas_call | solution.py:403
  83.3 1.6 %copy.8 = f32[1,256,128]{2,1,0:T(8,128)} copy(f32[1,256,128]{2,1,0:T(8,128)} %bitcast.5) | data formatting | bytes 262144

commit v6 on v5

--- a/solution.py
+++ b/solution.py
@@ -211,6 +211,7 @@
         )
 
     launch(remote(sbuf.at[0], sbuf.at[1], s_send.at[0], s_recv.at[0], z=up))
+    launch(remote(sbuf.at[0], sbuf.at[2], s_send.at[1], s_recv.at[1], z=zs[2]))
     for step in range(1, 4):
         to_holder(0, step - 1, step, jnp.int32(HOLDER[step]), yh + step < YH)
     other_rows = pl.ds(pl.multiple_of((1 - yl) * 128, 128), 128)
@@ -220,6 +221,16 @@
             fbuf.at[0, x, my_rows], fbuf.at[0, x, my_rows], f_send.at[0], f_recv.at[0, rep], yl=1 - yl
         )
     )
+    remote(sbuf.at[1], sbuf.at[1], s_send.at[0], s_recv.at[0], z=up).wait_recv()
+    for step in (2, 1, 3):
+        holder = jnp.where(yh + step >= YH, HOLDER[step], HOLDER[step + 4])
+        to_holder(1, 3 + step, step, holder)
+    to_holder(1, 3, 0, jnp.int32(HOLDER[4]), rep != HOLDER[4])
+
+    @pl.when(rep == HOLDER[4])
+    def _():
+        fbuf[1 + co, x, my_rows, :] = sbuf[1]
+
     for step in (2, 1, 3):
         launch(
             remote(
@@ -236,17 +247,6 @@
                 x=xs[step],
             )
         )
-
-    remote(sbuf.at[1], sbuf.at[1], s_send.at[0], s_recv.at[0], z=up).wait_recv()
-    launch(remote(sbuf.at[1], sbuf.at[2], s_send.at[1], s_recv.at[1], z=up))
-    for step in (2, 1, 3):
-        holder = jnp.where(yh + step >= YH, HOLDER[step], HOLDER[step + 4])
-        to_holder(1, 3 + step, step, holder)
-    to_holder(1, 3, 0, jnp.int32(HOLDER[4]), rep != HOLDER[4])
-
-    @pl.when(rep == HOLDER[4])
-    def _():
-        fbuf[1 + co, x, my_rows, :] = sbuf[1]
 
     remote(sbuf.at[2], sbuf.at[2], s_send.at[1], s_recv.at[1], z=up).wait_recv()
     for step in (2, 1, 3):

time: 85.1 us -> 84.2 us (0.989)
  Pallas kernels: 82.7 us -> 81.4 us
    pallas_call x1, Pallas kernels: 82.7 us -> 81.4 us  [per_device(): pl.pallas_call(kernel, out_shape=jax.ShapeDtypeStruct((256, NQ), F32), in...]
where the time goes in v6:
time: 84.2 us; the launch traced here: 83.6 us
  Pallas kernels  81.4 us (97%)
  local copies, waits for them, and re-layouts  1.57 us (2%)
    pallas_call x1, Pallas kernels, per_device(): pl.pallas_call(kernel, out_shape=jax.ShapeDtypeStruct((256, NQ), F32), in...  81.4 us

profile of v6, /device:TPU:1, one launch (start us, length us, event | category | flops | bytes accessed | tf_op | source)
XLA Modules:
  0.0 83.6 jit_solution(9948022285766261884)
XLA Ops:
  0.7 81.4 %gradient_density.1 = f32[256,128]{1,0:T(8,128)} custom-call(f32[1024,512]{1,0:T(8,128)} %bitcast.4, f32[32,512]{1,0:T(8,128)} %bitcast.6, f32[1024,128]{1,0:T(8,128)} %m_hbm.1, f32[1]{0:T(128)S(6)} %copy.7.occ_ref, f32[1,256]{1,0:T(1,128)} %bitcast.7), custom_call_target="tpu_custom_call" | custom-call | tf_op jit(solution)/shard_map/gradient_density/pallas_call | solution.py:403
  82.0 1.6 %copy.8 = f32[1,256,128]{2,1,0:T(8,128)} copy(f32[1,256,128]{2,1,0:T(8,128)} %bitcast.5) | data formatting | bytes 262144

commit v7 on v6

--- a/solution.py
+++ b/solution.py
@@ -350,17 +350,23 @@
             block = block + mm3((thi[order], tlo[order]), (jhi[order, xx], jlo[order, xx]))
         for half in range(YL):
             g[xx, half] = block[:, half * NQ : (half + 1) * NQ]
-        if step:
+        if step == 2:
+            launch(remote(g.at[xx, 1 - yl], tbuf.at[2], g_send.at[2, 0], g_recv.at[x, 1], yl=1 - yl))
+        elif step:
             to_column(step, 1 - yl, 0)
-    for step in (2, 1, 3):
+    for step in (1, 3):
         to_column(step, yl, 1)
+    remote(tbuf.at[2], tbuf.at[2], g_send.at[0, 0], g_recv.at[x, 1], co=1 - co).wait_recv()
+    tbuf[3] = g[xs[2], yl] + tbuf[2]
+    launch(remote(tbuf.at[3], grecv.at[x, yl], g_send.at[2, 1], g_recv.at[x, 1], x=xs[2]))
 
     def column_sum(half, index):
-        for step in (1, 3, 2):
+        steps = (1, 3, 2) if index else (1, 3)
+        for step in steps:
             block = grecv.at[xs[step], half]
             remote(block, block, g_send.at[0, 0], g_recv.at[xs[step], index], co=1 - co).wait_recv()
         result = g[x, half]
-        for step in (1, 2, 3):
+        for step in steps:
             result = result + grecv[xs[step], half]
         return result
 
@@ -422,7 +428,7 @@
             pltpu.VMEM((2, 8, 128), F32),
             pltpu.VMEM((X, YL, 256, NQ), F32),
             pltpu.VMEM((X, YL, 256, NQ), F32),
-            pltpu.VMEM((2, 256, NQ), F32),
+            pltpu.VMEM((4, 256, NQ), F32),
             dma((7,)), dma, dma, dma((2,)), dma((2,)), dma((2,)), dma((2,)), dma((4,)), dma((4,)),
             dma((2,)), dma((2,)), dma((8,)), dma((2, 8)), dma((11,)), dma((8,)), dma((8,)), dma((X, 2)), dma((X, 2)),
         ],

time: 84.2 us -> 83.7 us (level)
  no operation moved by 1% of the time
where the time goes in v7:
time: 83.7 us; the launch traced here: 83.4 us
  Pallas kernels  81.1 us (97%)
  local copies, waits for them, and re-layouts  1.57 us (2%)
    pallas_call x1, Pallas kernels, per_device(): pl.pallas_call(kernel, out_shape=jax.ShapeDtypeStruct((256, NQ), F32), in...  81.1 us

profile of v7, /device:TPU:1, one launch (start us, length us, event | category | flops | bytes accessed | tf_op | source)
XLA Modules:
  0.0 83.4 jit_solution(13780458739654058876)
XLA Ops:
  0.7 81.1 %gradient_density.1 = f32[256,128]{1,0:T(8,128)} custom-call(f32[1024,512]{1,0:T(8,128)} %bitcast.4, f32[32,512]{1,0:T(8,128)} %bitcast.6, f32[1024,128]{1,0:T(8,128)} %m_hbm.1, f32[1]{0:T(128)S(6)} %copy.7.occ_ref, f32[1,256]{1,0:T(1,128)} %bitcast.7), custom_call_target="tpu_custom_call" | custom-call | tf_op jit(solution)/shard_map/gradient_density/pallas_call | solution.py:409
  81.8 1.6 %copy.8 = f32[1,256,128]{2,1,0:T(8,128)} copy(f32[1,256,128]{2,1,0:T(8,128)} %bitcast.5) | data formatting | bytes 262144
